TPU v7x, 256 devices: a whole 4x4x8 slice. The times are simulated.
256 devices in a mesh: row: 32 (over y, z_hi, core), col: 8 (over z_lo, x).
Axes of the slice: x: 4, y: 4, z: 8 (z_hi: 4, z_lo: 2; z = z_hi * 2 + z_lo), core: 2. Of those that a mesh axis runs over, the one named last changes fastest.
Arguments:
- alignment: bfloat16 [64, 1024, 64], P(None, ('col', 'row')), may hold values from -6 to 6
- pair_rep: bfloat16 [1024, 1024, 128], P('row', 'col'), may hold values from -128 to 128
- outer_left: bfloat16 [64, 32], replicated, may hold values from -0.75 to 0.75
- outer_right: bfloat16 [64, 32], replicated, may hold values from -0.75 to 0.75
- outer_proj: bfloat16 [1024, 128], replicated, may hold values from -1.5 to 1.5
- outer_bias: float32 [128], replicated, may hold values from -3 to 3
- average_value: bfloat16 [64, 256], replicated, may hold values from -0.75 to 0.75
- average_gate: bfloat16 [64, 256], replicated, may hold values from -0.75 to 0.75
- average_logit: bfloat16 [128, 8], replicated, may hold values from -28 to 28
- average_out: bfloat16 [256, 64], replicated, may hold values from -1 to 1
- triangle_proj: bfloat16 [128, 512], replicated, may hold values from -0.5 to 0.5
- triangle_bias: bfloat16 [128, 4], replicated, may hold values from -0.5 to 0.5
Outputs:
- pair_new: bfloat16 [1024, 1024, 128], P('row', 'col')
- alignment_update: bfloat16 [64, 1024, 64], P(None, ('row', 'col'))
- triangle_inputs: bfloat16 [1024, 1024, 512], P(('col', 'row'))
- edge_bias: bfloat16 [4, 1024, 1024], P(None, ('col', 'row'))
All inputs are finite; a program needn't handle non-finite values.
Results may differ from a plain program's by a relative error of at most 0.02.
The roundings to bfloat16 on the way count: a program that leaves them out, or rounds other values in their place, can miss the bound.
Values may be sent and summed in bfloat16 or wider, within the bound.
No kernel may reach another device: no remote copies, remote signals or barrier semaphores. Data moves between devices by JAX's collectives and lax.ppermute only.
A program may use at most 64 MiB of HBM per device.

v0:
```python
import jax
import jax.numpy as jnp
from jax import lax
from jax.sharding import PartitionSpec as P


def broadcast(shard, axis, root):
    mine = lax.axis_index(axis) == root
    return lax.psum(jnp.where(mine, shard, jnp.zeros_like(shard)), axis)


def standardize(values):
    widened = values.astype(jnp.float32)
    centered = widened - jnp.mean(widened, axis=-1, keepdims=True)
    spread = jnp.mean(centered * centered, axis=-1, keepdims=True)
    return centered * lax.rsqrt(spread + 1e-05)


def per_device(
    alignment,
    pair_rep,
    outer_left,
    outer_right,
    outer_proj,
    outer_bias,
    average_value,
    average_gate,
    average_logit,
    average_out,
    triangle_proj,
    triangle_bias,
):
    row_devices = lax.axis_size("row")
    col_devices = lax.axis_size("col")
    local_row_index = lax.axis_index("row")
    col_index = lax.axis_index("col")
    sequence_count, slab_length, alignment_channel_width = alignment.shape
    row_window, cols_tile, pair_width = pair_rep.shape
    factor_width = outer_left.shape[1]
    head_count = average_logit.shape[1]
    value_width = average_value.shape[1]
    head_width = value_width // head_count
    alignment_layer_norm = standardize(alignment).astype(jnp.bfloat16)
    normalized_flat_rows = alignment_layer_norm.reshape(
        sequence_count, slab_length * alignment_channel_width
    )
    right_own = jnp.dot(
        alignment_layer_norm, outer_right, preferred_element_type=jnp.float32
    ).astype(jnp.bfloat16)
    value_own = jnp.dot(
        alignment_layer_norm, average_value, preferred_element_type=jnp.float32
    ).astype(jnp.bfloat16)
    normalized_columns, right_cols, value_cols = (
        lax.all_gather(normalized_flat_rows, "row", axis=1, tiled=True),
        lax.all_gather(
            right_own.reshape(sequence_count, slab_length * factor_width), "row", axis=1, tiled=True
        ),
        lax.all_gather(
            value_own.reshape(sequence_count, slab_length * value_width), "row", axis=1, tiled=True
        ),
    )
    right_cols = right_cols.reshape(sequence_count, cols_tile, factor_width)
    value_cols = value_cols.reshape(sequence_count, cols_tile, value_width)
    group_member_count = row_devices // col_devices
    start_position = local_row_index % group_member_count * (row_window * alignment_channel_width)
    local_rows = lax.dynamic_slice_in_dim(
        normalized_columns, start_position, row_window * alignment_channel_width, 1
    )
    norm_rows = broadcast(local_rows, "col", local_row_index // group_member_count).reshape(
        sequence_count, row_window, alignment_channel_width
    )
    left_rows = jnp.dot(norm_rows, outer_left, preferred_element_type=jnp.float32).astype(
        jnp.bfloat16
    )
    row_block = 8
    block_count = row_window // row_block
    left_blocks = jnp.transpose(
        left_rows.reshape(sequence_count, block_count, row_block * factor_width), (1, 0, 2)
    )
    right_flat = right_cols.reshape(sequence_count, cols_tile * factor_width)

    def pair_block(block_items):
        left_flat, pair_rows = block_items
        outer_sum = lax.dot_general(
            left_flat, right_flat, (((0,), (0,)), ((), ())), preferred_element_type=jnp.float32
        )
        outer_sum = jnp.transpose(
            outer_sum.reshape(row_block, factor_width, cols_tile, factor_width), (0, 2, 1, 3)
        )
        outer_mean = (
            outer_sum.reshape(row_block, cols_tile, factor_width * factor_width) / sequence_count
        ).astype(jnp.bfloat16)
        update = jnp.dot(outer_mean, outer_proj, preferred_element_type=jnp.float32)
        return (pair_rows.astype(jnp.float32) + update + outer_bias).astype(jnp.bfloat16)

    pair_new = lax.map(
        pair_block, (left_blocks, pair_rep.reshape(block_count, row_block, cols_tile, pair_width))
    )
    pair_new = pair_new.reshape(row_window, cols_tile, pair_width)
    pair_norm = standardize(pair_new).astype(jnp.bfloat16)
    logits = jnp.einsum("ijc,ch->hij", pair_norm, average_logit, preferred_element_type=jnp.float32)
    peak_values = lax.pmax(jnp.max(logits, axis=2), "col")
    weights = jnp.exp(logits - peak_values[:, :, None]).astype(jnp.bfloat16)
    denom_part = jnp.sum(weights.astype(jnp.float32), axis=2)
    value_heads = value_cols.reshape(sequence_count, cols_tile, head_count, head_width)
    numer_part = jnp.einsum(
        "hij,sjhc->ishc", weights, value_heads, preferred_element_type=jnp.float32
    )
    numer_part = numer_part.reshape(row_window, sequence_count, value_width)
    out_wide = average_out.astype(jnp.float32)
    numer_sub, denom_sub = (
        lax.psum_scatter(
            numer_part.astype(jnp.bfloat16), "col", scatter_dimension=0, tiled=True
        ).astype(jnp.float32),
        lax.psum_scatter(
            denom_part.astype(jnp.bfloat16), "col", scatter_dimension=1, tiled=True
        ).astype(jnp.float32),
    )
    sub_len = numer_sub.shape[0]
    norm_sub = lax.dynamic_slice_in_dim(norm_rows, col_index * sub_len, sub_len, 1)
    gate_vals = jax.nn.sigmoid(jnp.dot(norm_sub, average_gate, preferred_element_type=jnp.float32))
    gate_vals = gate_vals.reshape(sequence_count, sub_len, head_count, head_width)
    numer_moved = jnp.transpose(
        numer_sub.reshape(sub_len, sequence_count, head_count, head_width), (1, 0, 2, 3)
    )
    gated_vals = (gate_vals * numer_moved / jnp.transpose(denom_sub)[None, :, :, None]).reshape(
        sequence_count, sub_len, value_width
    )
    alignment_update = jnp.dot(gated_vals, out_wide, precision=lax.Precision.HIGHEST).astype(
        jnp.bfloat16
    )
    piece_len = cols_tile // row_devices
    shaped = pair_norm.reshape(row_window, row_devices, piece_len, pair_width)
    split_at = 3 * (triangle_proj.shape[1] // 4)
    turned = lax.all_to_all(shaped, "row", split_axis=1, concat_axis=0, tiled=True)[:, 0]
    projected = jnp.einsum("jic,cd->ijd", turned, triangle_proj, preferred_element_type=jnp.float32)
    inputs = jnp.concatenate(
        [projected[..., :split_at], jax.nn.sigmoid(projected[..., split_at:])], axis=-1
    ).astype(jnp.bfloat16)
    bias_rows = jnp.einsum(
        "jic,ch->ihj", turned, triangle_bias, preferred_element_type=jnp.float32
    ).astype(jnp.bfloat16)
    triangle_inputs, bias_rows = (inputs, bias_rows)
    edge_bias = jnp.transpose(bias_rows, (1, 0, 2))
    return (pair_new, alignment_update, triangle_inputs, edge_bias)


def solution(mesh):
    placed = (
        P(None, ("col", "row"), None),
        P("row", "col", None),
        P(),
        P(),
        P(),
        P(),
        P(),
        P(),
        P(),
        P(),
        P(),
        P(),
    )
    return jax.shard_map(
        per_device,
        mesh=mesh,
        in_specs=placed,
        out_specs=(
            P("row", "col", None),
            P(None, ("row", "col"), None),
            P(("col", "row"), None, None),
            P(None, ("col", "row"), None),
        ),
        check_vma=False,
    )
```

profile of v0, /device:TPU:16, one launch (start us, length us, event | category | flops | bytes accessed | tf_op | source)
XLA Modules:
  0.0 337.7 jit_solution(5402792686740338694)
XLA Ops:
  7.2 1.0 convert_reduce_fusion.1
  8.2 1.1 fusion.22
  9.3 1.0 fusion.23
  10.4 0.7 reshape.113
  11.2 53.5 %all-gather.3.cloned.1.call-done = bf16[64,8192]{1,0:T(8,128)(2,1)} async-done(((bf16[64,256]{1,0:T(8,128)(2,1)}), bf16[64,8192]{1,0:T(8,128)(2,1)}) %all-gather.3.cloned.1.call-update) | async-done | bytes 1048592 | tf_op jit(solution)/shard_map/all_gather | solution.py:54
  64.7 1.0 dynamic-slice_select_fusion
  66.3 1.0 copy.76
  68.4 41.0 %all_gather.10 = bf16[64,4096]{0,1:T(8,128)(2,1)S(1)} all-gather(bf16[64,128]{0,1:T(8,128)(2,1)S(1)} %bitcast.144), channel_id=1, replica_groups=mesh['row'=32,'col'=8] {'row'}, dimensions={1}, use_global_device_ids=true | all-gather | bytes 540672 | tf_op jit(solution)/shard_map/all_gather | solution.py:55
  109.4 37.8 %all-reduce.3.cloned.1.call-done = bf16[64,32,64]{2,0,1:T(8,128)(2,1)} async-done(((bf16[64,32,64]{2,0,1:T(8,128)(2,1)}), bf16[64,32,64]{2,0,1:T(8,128)(2,1)}) %all-reduce.3.cloned.1.call-update) | async-done | bytes 262160 | tf_op jit(solution)/shard_map/psum | solution.py:9
  147.1 1.6 convolution_convert_fusion
  148.8 17.9 %while.10 = (s32[]{:T(128)}, bf16[4,8,128,128]{3,2,1,0:T(8,128)(2,1)S(1)}, bf16[4,8,128,128]{3,2,1,0:T(8,128)(2,1)}, bf16[4,64,256]{1,2,0:T(8,128)(2,1)S(1)}, bf...) while((s32[]{:T(128)}, ...), condition=%wide.region_4.5_spmd, body=%wide.region_3.4_spmd.sunk | while | flops 405274624 | bytes 10846821 | solution.py:96
  148.8 1.1 copy.111
  149.9 0.7 fusion.59
  150.6 0.8 copy.112
  151.4 1.8 fusion.60
  153.3 1.1 copy.111
  154.4 0.7 fusion.59
  155.1 0.8 copy.112
  155.9 1.8 fusion.60
  157.8 1.1 copy.111
  158.9 0.7 fusion.59
  159.6 0.8 copy.112
  160.4 1.8 fusion.60
  162.2 1.1 copy.111
  163.4 0.7 fusion.59
  164.1 0.8 copy.112
  164.9 1.8 fusion.60
  166.7 1.9 copy.86
  169.2 1.3 multiply_reduce_fusion
  171.0 3.3 multiply_convert_fusion.1
  174.3 9.3 %all-to-all-start = ((bf16[32,32,4,128]{3,0,2,1:T(8,128)(2,1)}), bf16[32,32,4,128]{3,0,2,1:T(8,128)(2,1)S(1)}, u32[]{:S(2)}, u32[]{:S(2)}) async-start(bf16[32,32,4,128]{3,0,2,1:T(8,128)(2,1)} %multiply_convert_fusion.1), calls=%async_computation.1 | async-start | bytes 2097152 | tf_op jit(solution)/shard_map/all_to_all | solution.py:135
  183.6 2.1 fusion.41
  185.7 55.5 %pmax.7 = f32[8,32]{0,1:T(8,128)S(1)} all-reduce(f32[8,32]{0,1:T(8,128)S(1)} %get-tuple-element.76), channel_id=1, replica_groups=mesh['row'=32,'col'=8] {'col'}, use_global_device_ids=true, to_apply=%region_8.9 | all-reduce | flops 256 | bytes 2048 | tf_op jit(solution)/shard_map/pmax | solution.py:102
  241.4 8.4 %copy.81 = bf16[64,32768]{0,1:T(8,128)(2,1)} copy(bf16[64,32768]{1,0:T(8,128)(2,1)} %all-gather.5.cloned.1.call-done) | data formatting | bytes 8388608 | tf_op jit(solution)/shard_map/all_gather | solution.py:58
  249.8 14.8 %copy.82 = bf16[64,128,8,32]{1,3,0,2:T(8,128)(2,1)} copy(bf16[64,128,8,32]{0,3,2,1:T(8,128)(2,1)} %bitcast.130) | data formatting | bytes 8388608 | tf_op jit(solution)/shard_map/reshape;reshape | solution.py:105
  264.6 5.4 %convert_bitcast_fusion = bf16[32,64,8,32]{0,3,1,2:T(8,128)(2,1)} fusion(bf16[64,128,8,32]{1,3,0,2:T(8,128)(2,1)} %copy.82, bf16[8,32,128,1]{2,0,1,3:T(8,128)(2,1)S(1)} %fusion.33), kind=kOutput, calls=%fused_computation.12 | convolution fusion | flops 134742016 | bytes 5308416 | tf_op jit(solution)/shard_map/hij,sjhc->ishc/dot_general | solution.py:106
  269.9 8.1 %copy.84 = bf16[32,64,8,32]{1,3,2,0:T(8,128)(2,1)} copy(bf16[32,64,8,32]{0,3,1,2:T(8,128)(2,1)} %convert_bitcast_fusion) | data formatting | bytes 2097152 | tf_op jit(solution)/shard_map/convert_element_type | solution.py:113
  280.0 1.0 fusion.13
  281.4 18.6 %all-reduce = bf16[8,32]{0,1:T(8,128)(2,1)S(1)} all-reduce(bf16[8,32]{0,1:T(8,128)(2,1)S(1)} %fusion.32), channel_id=3, replica_groups=mesh['row'=32,'col'=8] {'col'}, use_global_device_ids=true, to_apply=%region_11.12.clone | all-reduce | flops 256 | bytes 1024
  300.1 1.0 copy-done.2
  301.1 1.3 copy.89
  302.4 1.3 convolution_bitcast_fusion
  304.8 2.4 pad_maximum_fusion
  307.1 6.2 %copy.92 = bf16[4,1024,512]{2,1,0:T(8,128)(2,1)} copy(bf16[4,1024,512]{1,2,0:T(8,128)(2,1)} %pad_maximum_fusion) | data formatting | bytes 8388608
  313.7 0.6 copy.93
  314.4 14.4 %reduce-scatter.2.cloned.1.call-done = bf16[4,64,256]{1,2,0:T(8,128)(2,1)} async-done(((bf16[32,64,256]{1,2,0:T(8,128)(2,1)}), bf16[4,64,256]{1,2,0:T(8,128)(2,1)}) %reduce-scatter.2.cloned.1.call-update) | async-done | bytes 131088 | tf_op jit(solution)/shard_map/reduce_scatter | solution.py:112
  328.8 1.1 fusion.19
  330.5 0.7 copy.91
  (62 shorter events, 6.6 us)
Async XLA Ops:
  7.2 295.2 %copy-start = (bf16[128,512]{1,0:T(8,128)(2,1)S(1)}, bf16[128,512]{1,0:T(8,128)(2,1)}, u32[]{:S(2)}) copy-start(bf16[128,512]{1,0:T(8,128)(2,1)} %param.24) | copy-start | bytes 393220
  7.2 60.2 %copy-start.3 = (bf16[64,256]{1,0:T(8,128)(2,1)S(1)}, bf16[64,256]{1,0:T(8,128)(2,1)}, u32[]{:S(2)}) copy-start(bf16[64,256]{1,0:T(8,128)(2,1)} %param.20) | copy-start | bytes 98308
  7.2 57.5 %all-gather.3.cloned.1.call-start = ((), (), s32[]{:S(2)}) async-start(), calls=%async_computation.2 | async-start | bytes 1081344 | tf_op jit(solution)/shard_map/all_gather | solution.py:54
  8.2 60.0 %copy-start.6 = (bf16[64,32]{0,1:T(8,128)(2,1)S(1)}, bf16[64,32]{0,1:T(8,128)(2,1)}, u32[]{:S(2)}) copy-start(bf16[64,32]{0,1:T(8,128)(2,1)} %param.17) | copy-start | bytes 12292
  11.1 136.0 %all-reduce.3.cloned.1.call-start = ((), (), s32[]{:S(2)}) async-start(), calls=%async_computation.3 | async-start | bytes 1048576 | tf_op jit(solution)/shard_map/psum | solution.py:9
  65.7 81.4 %copy-start.5 = (bf16[64,32]{0,1:T(8,128)(2,1)S(1)}, bf16[64,32]{0,1:T(8,128)(2,1)}, u32[]{:S(2)}) copy-start(bf16[64,32]{0,1:T(8,128)(2,1)} %param.16) | copy-start | bytes 12292
  66.3 82.5 %copy-start.8 = (bf16[1024,128]{1,0:T(8,128)(2,1)S(1)}, bf16[1024,128]{1,0:T(8,128)(2,1)}, u32[]{:S(2)}) copy-start(bf16[1024,128]{1,0:T(8,128)(2,1)} %param.18) | copy-start | bytes 786436
  66.3 82.5 %copy-start.11 = (f32[128]{0:T(128)S(1)}, f32[128]{0:T(128)}, u32[]{:S(2)}) copy-start(f32[128]{0:T(128)} %param.19) | copy-start | bytes 1540
  67.3 174.1 %all-gather.5.cloned.1.call-start = ((), (), s32[]{:S(2)}) async-start(), calls=%async_computation.4 | async-start | bytes 4325376 | tf_op jit(solution)/shard_map/all_gather | solution.py:58
  166.7 16.9 %copy-start.1 = (bf16[4,8,128,128]{3,2,1,0:T(8,128)(2,1)}, bf16[4,8,128,128]{3,2,1,0:T(8,128)(2,1)S(1)}, u32[]{:S(2)}) copy-start(bf16[4,8,128,128]{3,2,1,0:T(8,128)(2,1)S(1)} %get-tuple-element.41) | copy-start | bytes 3145732
  171.0 12.6 %copy-start.10 = (bf16[128,8]{0,1:T(8,128)(2,1)S(1)}, bf16[128,8]{0,1:T(8,128)(2,1)}, u32[]{:S(2)}) copy-start(bf16[128,8]{0,1:T(8,128)(2,1)} %param.22) | copy-start | bytes 6148
  174.3 125.8 %all-to-all-start = ((bf16[32,32,4,128]{3,0,2,1:T(8,128)(2,1)}), bf16[32,32,4,128]{3,0,2,1:T(8,128)(2,1)S(1)}, u32[]{:S(2)}, u32[]{:S(2)}) async-start(bf16[32,32,4,128]{3,0,2,1:T(8,128)(2,1)} %multiply_convert_fusion.1), calls=%async_computation.1 | async-start | bytes 2097152 | tf_op jit(solution)/shard_map/all_to_all | solution.py:135
  183.5 145.3 %reduce-scatter.2.cloned.1.call-start = ((), (), s32[]{:S(2)}) async-start(), calls=%async_computation.5 | async-start | bytes 2359296 | tf_op jit(solution)/shard_map/reduce_scatter | solution.py:112
  278.0 0.7 copy-start.12
  278.1 1.9 copy-start.9
  300.1 1.0 copy-start.2
  307.1 6.2 %copy-start.7 = (bf16[128,4]{0,1:T(4,128)(2,1)S(1)}, bf16[128,4]{0,1:T(4,128)(2,1)}, u32[]{:S(2)}) copy-start(bf16[128,4]{0,1:T(4,128)(2,1)} %param.25) | copy-start | bytes 3076
  313.4 16.5 %copy-start.4 = (bf16[256,64]{0,1:T(8,128)(2,1)S(1)}, bf16[256,64]{0,1:T(8,128)(2,1)}, u32[]{:S(2)}) copy-start(bf16[256,64]{0,1:T(8,128)(2,1)} %param.23) | copy-start | bytes 98308
Sparse Core Ops, SparseCore 0:
  11.3 53.4 all-gather.2
  67.9 79.1 all-reduce.2
  149.8 74.9 all-gather.4
  278.2 50.5 reduce-scatter.1
where the time goes:
time: 339 us; the launch traced here: 338 us
  blocking collectives  115 us (34%)
  waiting for transfers between devices  106 us (31%)
  local copies, waits for them, and re-layouts  56.4 us (17%)
  matrix products  22.7 us (7%)
  between operations  14.8 us (4%)
  other arithmetic  13.3 us (4%)
  starting transfers between devices  9.42 us (3%)
    pmax x1, blocking collectives, per_device(): peak_values = lax.pmax(jnp.max(logits, axis=2), 'col')  55.5 us
    all_gather x1, waiting for transfers between devices, per_device(): lax.all_gather(normalized_flat_rows, 'row', axis=1, tiled=True)  53.5 us
    all_gather x1, blocking collectives, per_device(): lax.all_gather(right_own.reshape(sequence_count, slab_length * factor_wid...  41 us
    psum x1, waiting for transfers between devices, broadcast(): return lax.psum(jnp.where(mine, shard, jnp.zeros_like(shard)), axis)  37.8 us
    unnamed x1, blocking collectives  18.6 us
    another operation x1, local copies, waits for them, and re-layouts, per_device(): value_cols.reshape(sequence_count, cols_tile, head_count, head_width)  14.8 us
    reduce_scatter x1, waiting for transfers between devices, per_device(): lax.psum_scatter(numer_part.astype(jnp.bfloat16), 'col', scatter_dimensio...  14.4 us
    unnamed x30, local copies, waits for them, and re-layouts  9.84 us
  transfers between devices with their start and end apart: 5, of which 3 were waited for; matrix products, arithmetic and copies ran while one was open for 24% of the time, Pallas kernels for 0%

commit v1 on v0

--- a/solution.py
+++ b/solution.py
@@ -51,7 +51,10 @@
         alignment_layer_norm, average_value, preferred_element_type=jnp.float32
     ).astype(jnp.bfloat16)
     normalized_columns, right_cols, value_cols = (
-        lax.all_gather(normalized_flat_rows, "row", axis=1, tiled=True),
+        jnp.concatenate(
+            lax.all_to_all(jnp.stack([normalized_flat_rows] * lax.axis_size("row")), "row", 0, 0),
+            axis=1,
+        ),
         lax.all_gather(
             right_own.reshape(sequence_count, slab_length * factor_width), "row", axis=1, tiled=True
         ),

time: 339 us -> 317 us (0.935)
  waiting for transfers between devices: 106 us -> 81.1 us
  starting transfers between devices: 9.42 us -> 22 us
  blocking collectives: 115 us -> 103 us
    all_gather x1 -> x0, waiting for transfers between devices: 53.5 us -> none  [per_device(): lax.all_gather(normalized_flat_rows, 'row', axis=1, tiled=True)]
    all_to_all x0 -> x1, waiting for transfers between devices: none -> 27.2 us  [per_device(): lax.all_to_all(jnp.stack([normalized_flat_rows] * lax.axis_size('row')),...]
    all_to_all x0 -> x1, starting transfers between devices: none -> 11.6 us  [per_device(): lax.all_to_all(jnp.stack([normalized_flat_rows] * lax.axis_size('row')),...]
    pmax x1, blocking collectives: 55.5 us -> 46.3 us  [per_device(): peak_values = lax.pmax(jnp.max(logits, axis=2), 'col')]
    psum x1, waiting for transfers between devices: 37.8 us -> 41.2 us  [broadcast(): return lax.psum(jnp.where(mine, shard, jnp.zeros_like(shard)), axis)]
  transfers between devices with their start and end apart: 5 -> 5, of which waited for: 3 -> 3; matrix products, arithmetic and copies ran while one was open for 24% -> 26% of each run, Pallas kernels for 0% -> 0%
where the time goes in v1:
time: 317 us; the launch traced here: 315 us
  blocking collectives  103 us (32%)
  waiting for transfers between devices  81.1 us (26%)
  local copies, waits for them, and re-layouts  56.9 us (18%)
  matrix products  22.7 us (7%)
  starting transfers between devices  22 us (7%)
  between operations  16.6 us (5%)
  other arithmetic  12.4 us (4%)
    pmax x1, blocking collectives, per_device(): peak_values = lax.pmax(jnp.max(logits, axis=2), 'col')  46.3 us
    psum x1, waiting for transfers between devices, broadcast(): return lax.psum(jnp.where(mine, shard, jnp.zeros_like(shard)), axis)  41.2 us
    all_gather x1, blocking collectives, per_device(): lax.all_gather(right_own.reshape(sequence_count, slab_length * factor_wid...  40.3 us
    all_to_all x1, waiting for transfers between devices, per_device(): lax.all_to_all(jnp.stack([normalized_flat_rows] * lax.axis_size('row')),...  27.2 us
    unnamed x1, blocking collectives  16.7 us
    another operation x1, local copies, waits for them, and re-layouts, per_device(): value_cols.reshape(sequence_count, cols_tile, head_count, head_width)  14.8 us
    reduce_scatter x1, waiting for transfers between devices, per_device(): lax.psum_scatter(numer_part.astype(jnp.bfloat16), 'col', scatter_dimensio...  12.7 us
    all_to_all x1, starting transfers between devices, per_device(): lax.all_to_all(jnp.stack([normalized_flat_rows] * lax.axis_size('row')),...  11.6 us
  transfers between devices with their start and end apart: 5, of which 3 were waited for; matrix products, arithmetic and copies ran while one was open for 26% of the time, Pallas kernels for 0%

profile of v1, /device:TPU:16, one launch (start us, length us, event | category | flops | bytes accessed | tf_op | source)
XLA Modules:
  0.0 315.2 jit_solution(9470477640377772255)
XLA Ops:
  8.0 1.0 convert_reduce_fusion.1
  9.0 1.1 fusion.22
  10.1 1.0 fusion.23
  11.3 1.1 stack.3
  12.4 11.6 %all-to-all-start = ((bf16[32,64,256]{2,1,0:T(8,128)(2,1)}), bf16[32,64,256]{2,1,0:T(8,128)(2,1)S(1)}, u32[]{:S(2)}, u32[]{:S(2)}) async-start(bf16[32,64,256]{2,1,0:T(8,128)(2,1)} %stack.3), calls=%async_computation | async-start | bytes 2097152 | tf_op jit(solution)/shard_map/all_to_all | solution.py:55
  24.1 27.2 %all-to-all-done = bf16[32,64,256]{2,1,0:T(8,128)(2,1)S(1)} async-done(((bf16[32,64,256]{2,1,0:T(8,128)(2,1)}), bf16[32,64,256]{2,1,0:T(8,128)(2,1)S(1)}, u32[]{:S(2)}, u32[]{:S(2)}) %all-to-all-start) | async-done | bytes 1048608 | tf_op jit(solution)/shard_map/all_to_all | solution.py:55
  52.0 1.0 copy.98
  53.2 0.7 copy.125
  54.1 40.3 %all_gather.6 = bf16[64,4096]{0,1:T(8,128)(2,1)S(1)} all-gather(bf16[64,128]{0,1:T(8,128)(2,1)S(1)} %bitcast.149), channel_id=1, replica_groups=mesh['row'=32,'col'=8] {'row'}, dimensions={1}, use_global_device_ids=true | all-gather | bytes 540672 | tf_op jit(solution)/shard_map/all_gather | solution.py:58
  94.4 41.2 %all-reduce.3.cloned.1.call-done = bf16[64,32,64]{2,0,1:T(8,128)(2,1)} async-done(((bf16[64,32,64]{2,0,1:T(8,128)(2,1)}), bf16[64,32,64]{2,0,1:T(8,128)(2,1)}) %all-reduce.3.cloned.1.call-update) | async-done | bytes 262160 | tf_op jit(solution)/shard_map/psum | solution.py:9
  135.6 1.6 convolution_convert_fusion
  137.3 17.9 %while.10 = (s32[]{:T(128)}, bf16[4,8,128,128]{3,2,1,0:T(8,128)(2,1)S(1)}, bf16[4,8,128,128]{3,2,1,0:T(8,128)(2,1)}, bf16[4,64,256]{1,2,0:T(8,128)(2,1)S(1)}, bf...) while((s32[]{:T(128)}, ...), condition=%wide.region_4.5_spmd, body=%wide.region_3.4_spmd.sunk | while | flops 405274624 | bytes 10846821 | solution.py:99
  137.3 1.1 copy.134
  138.4 0.7 fusion.59
  139.1 0.8 copy.135
  139.9 1.8 fusion.60
  141.8 1.1 copy.134
  142.9 0.7 fusion.59
  143.6 0.8 copy.135
  144.4 1.8 fusion.60
  146.2 1.1 copy.134
  147.4 0.7 fusion.59
  148.0 0.8 copy.135
  148.9 1.8 fusion.60
  150.7 1.1 copy.134
  151.8 0.7 fusion.59
  152.5 0.8 copy.135
  153.3 1.8 fusion.60
  155.2 1.9 copy.108
  157.6 1.3 multiply_reduce_fusion
  159.5 3.3 %multiply_convert_fusion.1 = bf16[32,32,4,128]{3,0,2,1:T(8,128)(2,1)} fusion(f32[32,32,4,128]{3,0,2,1:T(8,128)} %bitcast.139, f32[32,32,4]{0,2,1:T(4,128)S(1)} %rsqrt.26, f32[32,32,4]{0,2,1:T(4,128)S(1)} %div.52), kind=kLoop, calls=%fused_computation.18 | loop fusion | flops 1572864 | bytes 3178496 | tf_op jit(solution)/shard_map/convert_element_type | solution.py:103
  162.7 10.2 %all-to-all-start.1 = ((bf16[32,32,4,128]{3,0,2,1:T(8,128)(2,1)}), bf16[32,32,4,128]{3,0,2,1:T(8,128)(2,1)S(1)}, u32[]{:S(2)}, u32[]{:S(2)}) async-start(bf16[32,32,4,128]{3,0,2,1:T(8,128)(2,1)} %multiply_convert_fusion.1), calls=%async_computation.2 | async-start | bytes 2097152 | tf_op jit(solution)/shard_map/all_to_all | solution.py:138
  173.1 2.1 fusion.41
  175.2 46.3 %pmax.7 = f32[8,32]{0,1:T(8,128)S(1)} all-reduce(f32[8,32]{0,1:T(8,128)S(1)} %get-tuple-element.80), channel_id=1, replica_groups=mesh['row'=32,'col'=8] {'col'}, use_global_device_ids=true, to_apply=%region_8.9 | all-reduce | flops 256 | bytes 2048 | tf_op jit(solution)/shard_map/pmax | solution.py:105
  221.6 8.4 %copy.103 = bf16[64,32768]{0,1:T(8,128)(2,1)} copy(bf16[64,32768]{1,0:T(8,128)(2,1)} %all-gather.2.cloned.1.call-done) | data formatting | bytes 8388608 | tf_op jit(solution)/shard_map/all_gather | solution.py:61
  230.0 14.8 %copy.104 = bf16[64,128,8,32]{1,3,0,2:T(8,128)(2,1)} copy(bf16[64,128,8,32]{0,3,2,1:T(8,128)(2,1)} %bitcast.133) | data formatting | bytes 8388608 | tf_op jit(solution)/shard_map/reshape;reshape | solution.py:108
  244.8 5.4 %convert_bitcast_fusion = bf16[32,64,8,32]{0,3,1,2:T(8,128)(2,1)} fusion(bf16[64,128,8,32]{1,3,0,2:T(8,128)(2,1)} %copy.104, bf16[8,32,128,1]{2,0,1,3:T(8,128)(2,1)S(1)} %fusion.33), kind=kOutput, calls=%fused_computation.12 | convolution fusion | flops 134742016 | bytes 5308416 | tf_op jit(solution)/shard_map/hij,sjhc->ishc/dot_general | solution.py:109
  250.2 8.1 %copy.106 = bf16[32,64,8,32]{1,3,2,0:T(8,128)(2,1)} copy(bf16[32,64,8,32]{0,3,1,2:T(8,128)(2,1)} %convert_bitcast_fusion) | data formatting | bytes 2097152 | tf_op jit(solution)/shard_map/convert_element_type | solution.py:116
  260.2 1.0 fusion.13
  261.7 16.7 %all-reduce = bf16[8,32]{0,1:T(8,128)(2,1)S(1)} all-reduce(bf16[8,32]{0,1:T(8,128)(2,1)S(1)} %fusion.32), channel_id=3, replica_groups=mesh['row'=32,'col'=8] {'col'}, use_global_device_ids=true, to_apply=%region_11.12.clone | all-reduce | flops 256 | bytes 1024
  278.4 1.0 copy-done.2
  279.4 1.3 copy.111
  280.7 1.3 convolution_bitcast_fusion
  283.1 2.4 pad_maximum_fusion
  285.5 6.2 %copy.114 = bf16[4,1024,512]{2,1,0:T(8,128)(2,1)} copy(bf16[4,1024,512]{1,2,0:T(8,128)(2,1)} %pad_maximum_fusion) | data formatting | bytes 8388608
  292.7 12.7 %reduce-scatter.2.cloned.1.call-done = bf16[4,64,256]{1,2,0:T(8,128)(2,1)} async-done(((bf16[32,64,256]{1,2,0:T(8,128)(2,1)}), bf16[4,64,256]{1,2,0:T(8,128)(2,1)}) %reduce-scatter.2.cloned.1.call-update) | async-done | bytes 131088 | tf_op jit(solution)/shard_map/reduce_scatter | solution.py:115
  305.4 1.1 fusion.19
  307.1 0.7 copy.113
  (63 shorter events, 6.8 us)
Async XLA Ops:
  8.0 272.7 %copy-start = (bf16[128,512]{1,0:T(8,128)(2,1)S(1)}, bf16[128,512]{1,0:T(8,128)(2,1)}, u32[]{:S(2)}) copy-start(bf16[128,512]{1,0:T(8,128)(2,1)} %param.24) | copy-start | bytes 393220
  12.4 38.9 %all-to-all-start = ((bf16[32,64,256]{2,1,0:T(8,128)(2,1)}), bf16[32,64,256]{2,1,0:T(8,128)(2,1)S(1)}, u32[]{:S(2)}, u32[]{:S(2)}) async-start(bf16[32,64,256]{2,1,0:T(8,128)(2,1)} %stack.3), calls=%async_computation | async-start | bytes 2097152 | tf_op jit(solution)/shard_map/all_to_all | solution.py:55
  24.0 111.6 %all-reduce.3.cloned.1.call-start = ((), (), s32[]{:S(2)}) async-start(), calls=%async_computation.3 | async-start | bytes 1048576 | tf_op jit(solution)/shard_map/psum | solution.py:9
  51.2 1.8 copy-start.3
  51.3 2.6 copy-start.6
  51.4 84.2 %copy-start.5 = (bf16[64,32]{0,1:T(8,128)(2,1)S(1)}, bf16[64,32]{0,1:T(8,128)(2,1)}, u32[]{:S(2)}) copy-start(bf16[64,32]{0,1:T(8,128)(2,1)} %param.16) | copy-start | bytes 12292
  51.9 85.3 %copy-start.8 = (bf16[1024,128]{1,0:T(8,128)(2,1)S(1)}, bf16[1024,128]{1,0:T(8,128)(2,1)}, u32[]{:S(2)}) copy-start(bf16[1024,128]{1,0:T(8,128)(2,1)} %param.18) | copy-start | bytes 786436
  51.9 85.3 %copy-start.11 = (f32[128]{0:T(128)S(1)}, f32[128]{0:T(128)}, u32[]{:S(2)}) copy-start(f32[128]{0:T(128)} %param.19) | copy-start | bytes 1540
  53.0 168.7 %all-gather.2.cloned.1.call-start = ((), (), s32[]{:S(2)}) async-start(), calls=%async_computation.4 | async-start | bytes 4325376 | tf_op jit(solution)/shard_map/all_gather | solution.py:61
  155.2 17.9 %copy-start.1 = (bf16[4,8,128,128]{3,2,1,0:T(8,128)(2,1)}, bf16[4,8,128,128]{3,2,1,0:T(8,128)(2,1)S(1)}, u32[]{:S(2)}) copy-start(bf16[4,8,128,128]{3,2,1,0:T(8,128)(2,1)S(1)} %get-tuple-element.41) | copy-start | bytes 3145732
  159.4 13.6 %copy-start.10 = (bf16[128,8]{0,1:T(8,128)(2,1)S(1)}, bf16[128,8]{0,1:T(8,128)(2,1)}, u32[]{:S(2)}) copy-start(bf16[128,8]{0,1:T(8,128)(2,1)} %param.22) | copy-start | bytes 6148
  162.7 115.7 %all-to-all-start.1 = ((bf16[32,32,4,128]{3,0,2,1:T(8,128)(2,1)}), bf16[32,32,4,128]{3,0,2,1:T(8,128)(2,1)S(1)}, u32[]{:S(2)}, u32[]{:S(2)}) async-start(bf16[32,32,4,128]{3,0,2,1:T(8,128)(2,1)} %multiply_convert_fusion.1), calls=%async_computation.2 | async-start | bytes 2097152 | tf_op jit(solution)/shard_map/all_to_all | solution.py:138
  173.0 132.4 %reduce-scatter.2.cloned.1.call-start = ((), (), s32[]{:S(2)}) async-start(), calls=%async_computation.5 | async-start | bytes 2359296 | tf_op jit(solution)/shard_map/reduce_scatter | solution.py:115
  258.3 0.7 copy-start.12
  258.3 1.9 copy-start.9
  278.4 1.0 copy-start.2
  285.5 6.2 %copy-start.7 = (bf16[128,4]{0,1:T(4,128)(2,1)S(1)}, bf16[128,4]{0,1:T(4,128)(2,1)}, u32[]{:S(2)}) copy-start(bf16[128,4]{0,1:T(4,128)(2,1)} %param.25) | copy-start | bytes 3076
  291.7 14.8 %copy-start.4 = (bf16[256,64]{0,1:T(8,128)(2,1)S(1)}, bf16[256,64]{0,1:T(8,128)(2,1)}, u32[]{:S(2)}) copy-start(bf16[256,64]{0,1:T(8,128)(2,1)} %param.23) | copy-start | bytes 98308
Sparse Core Ops, SparseCore 0:
  53.1 82.4 all-reduce.2
  258.4 46.9 reduce-scatter.1
Sparse Core Ops, SparseCore 1:
  56.1 59.8 all-gather.1
